TPU v7x, 32 devices: a whole 2x2x4 slice. The times are simulated.
32 devices in a mesh: grp: 4 (over x, core), clu: 8 (over z, y).
Axes of the slice: x: 2, y: 2, z: 4, core: 2. Of those that a mesh axis runs over, the one named last changes fastest.
Arguments:
- radiosity: float32 [128, 3, 128], P(('grp', 'clu')), may hold values from 0 to 3
- form_factors: float32 [4096, 128, 128], P(('grp', 'clu')), may hold values from 0.01 to 16
- source_device: int32 [4096, 1], P(('grp', 'clu')), may hold values from 0 to 31; in each aligned block of 128 rows (0 to 127, 128 to 255, ...) at most 8 rows name the same one
- source_slot: int32 [4096], P(('grp', 'clu')), may hold values from 0 to 3
- receiver_slot: int32 [4096], P(('grp', 'clu')), may hold values from 0 to 3
- emission: float32 [128, 3, 128], P(('grp', 'clu')), may hold values from 0.1 to 2
- reflectance: float32 [128, 3, 128], P(('grp', 'clu')), may hold values from 0.3 to 0.9
- patch_area: float32 [128, 128], P(('grp', 'clu')), may hold values from 0.5 to 2
- cluster_group: int32 [128], P(('grp', 'clu')), may hold values from 0 to 15, as said below
- group_coupling: float32 [16, 16], replicated, may hold values from 0 to 1
- ambient: float32 [3], replicated, may hold values from 0.2 to 1
Outputs:
- radiosity_new: float32 [128, 3, 128], P(('grp', 'clu'))
- group_radiosity: float32 [16, 3], replicated
Inputs may be any that keep to these rules, and one draw needn't show every extreme that they name: `source_device`: the rows of one device name each source device at most 8 times. `cluster_group`: each group node has exactly 8 clusters.
All inputs are finite; a program needn't handle non-finite values.
Results may differ from a plain program's by a relative error of at most 0.00005.
Values sent between devices are 32-bit elements; how exact they have to be, the bound alone decides.
No kernel may reach another device: no remote copies, remote signals or barrier semaphores. Data moves between devices by JAX's collectives and lax.ppermute only.
A program may use at most 64 MiB of HBM per device.

v0:
```python
import jax
import jax.numpy as jnp
from jax import lax
from jax.sharding import PartitionSpec as P


def cluster_sums(field, patch_area):
    return jnp.einsum("kci,ki->kc", field, patch_area, precision=lax.Precision.HIGHEST)


def on_device(
    radiosity,
    form_factors,
    source_device,
    source_slot,
    receiver_slot,
    emission,
    reflectance,
    patch_area,
    cluster_group,
    group_coupling,
    ambient,
):
    clusters_here = radiosity.shape[0]
    count = form_factors.shape[0]
    width = form_factors.shape[1]
    groups_all = group_coupling.shape[0]
    devices = lax.axis_size("grp") * lax.axis_size("clu")
    scale = 2.0 * clusters_here / (width * count)
    sources = source_device[:, 0]
    capacity = max(2, 2 * count // devices)
    order = jnp.arange(count, dtype=jnp.int32)
    earlier = (sources[None, :] == sources[:, None]) & (order[None, :] < order[:, None])
    ranking = jnp.sum(earlier.astype(jnp.int32), axis=1)
    position = sources * capacity + ranking
    wanted = jnp.zeros((devices * capacity,), jnp.int32).at[position].set(source_slot + 1)
    asked = lax.all_to_all(
        wanted.reshape(devices, capacity), ("grp", "clu"), split_axis=0, concat_axis=0, tiled=True
    ).reshape(devices * capacity)
    valid = (asked > 0).astype(jnp.float32)
    answer = jnp.take(radiosity, jnp.maximum(asked - 1, 0), axis=0) * valid[:, None, None]
    returned = lax.all_to_all(
        answer.reshape(devices, capacity, 3, width),
        ("grp", "clu"),
        split_axis=0,
        concat_axis=0,
        tiled=True,
    ).reshape(devices * capacity, 3, width)
    fetched = jnp.take(returned, position, axis=0)
    contribution = (
        jnp.einsum("lij,lcj->lci", form_factors, fetched, precision=lax.Precision.HIGHEST) * scale
    )
    receiver_table = (
        receiver_slot[:, None] == jnp.arange(clusters_here, dtype=jnp.int32)[None, :]
    ).astype(jnp.float32)
    irradiance = jnp.einsum(
        "lk,lci->kci", receiver_table, contribution, precision=lax.Precision.HIGHEST
    )
    group_table = (
        cluster_group[:, None] == jnp.arange(groups_all, dtype=jnp.int32)[None, :]
    ).astype(jnp.float32)
    local_sum = jnp.dot(
        group_table.T, cluster_sums(radiosity, patch_area), precision=lax.Precision.HIGHEST
    )
    local_area = jnp.dot(
        group_table.T, jnp.sum(patch_area, axis=1), precision=lax.Precision.HIGHEST
    )
    group_sum, group_area = lax.psum((local_sum, local_area), ("grp", "clu"))
    old_group = group_sum / group_area[:, None]
    old_root = jnp.sum(group_sum, axis=0) / jnp.sum(group_area)
    group_irradiance = jnp.dot(
        group_coupling / groups_all, old_group, precision=lax.Precision.HIGHEST
    )
    coarse = (
        jnp.dot(group_table, group_irradiance, precision=lax.Precision.HIGHEST)
        + (ambient * old_root)[None, :]
    )
    radiosity_new = emission + reflectance * (irradiance + coarse[:, :, None])
    new_local = jnp.dot(
        group_table.T, cluster_sums(radiosity_new, patch_area), precision=lax.Precision.HIGHEST
    )
    new_sum = lax.psum(new_local, ("grp", "clu"))
    return (radiosity_new, new_sum / group_area[:, None])


def solution(mesh):
    return jax.shard_map(
        on_device,
        mesh=mesh,
        in_specs=(
            P(("grp", "clu"), None, None),
            P(("grp", "clu"), None, None),
            P(("grp", "clu"), None),
            P(("grp", "clu")),
            P(("grp", "clu")),
            P(("grp", "clu"), None, None),
            P(("grp", "clu"), None, None),
            P(("grp", "clu"), None),
            P(("grp", "clu")),
            P(),
            P(),
        ),
        out_specs=(P(("grp", "clu"), None, None), P()),
        check_vma=False,
    )
```

profile of v0, /device:TPU:0, one launch (start us, length us, event | category | flops | bytes accessed | tf_op | source)
XLA Modules:
  0.0 133.1 jit_solution(4761366920443387148)
XLA Ops:
  0.6 0.0 copy-start
  0.6 0.9 convert_reduce_fusion
  1.6 0.7 and_bitcast_fusion
  2.2 0.7 broadcast_add_fusion
  2.9 1.0 scatter_custom_fusion
  3.9 0.7 all_to_all.9
  4.5 7.3 %all-to-all-start = ((s32[32,1,8]{2,1,0:T(1,128)}), s32[32,1,8]{2,1,0:T(1,128)S(1)}, u32[]{:S(2)}, u32[]{:S(2)}) async-start(s32[32,1,8]{2,1,0:T(1,128)} %bitcast.5), calls=%async_computation | async-start | bytes 32768 | tf_op jit(solution)/shard_map/all_to_all | solution.py:37
  11.9 0.0 copy-done
  11.9 0.1 reduce_sum.40
  12.0 0.8 fusion.12
  12.9 0.9 fusion.18
  13.7 0.8 convolution_bitcast_fusion
  14.5 40.4 %all-reduce = (f32[16,3]{0,1:T(4,128)S(1)}, f32[16]{0:T(128)S(1)}) all-reduce(f32[16,3]{0,1:T(4,128)S(1)} %fusion.18, f32[16]{0:T(128)S(1)} %convolution_bitcast_fusion), channel_id=1, replica_groups=mesh['grp'=4,'clu'=8] {'grp','clu'}, use_global_device_ids=true, to_apply=%region_2.3 | all-reduce | flops 64 | bytes 512 | tf_op jit(solution)/shard_map/psum | solution.py:68
  54.9 0.6 reduce_sum.42
  55.5 0.1 reduce_sum.41
  55.7 0.0 all-to-all-done
  55.7 0.1 copy.28
  55.7 0.1 copy.33
  55.8 0.1 copy.29
  55.9 0.1 copy.30
  56.0 0.1 reshape.76
  56.1 0.0 copy-start.1
  56.1 0.0 copy-start.2
  56.1 0.0 copy-start.4
  56.1 0.0 copy-start.5
  56.1 2.1 %gather_fusion = f32[256,3,128]{2,0,1:T(8,128)S(1)} fusion(f32[4,3,128]{2,0,1:T(4,128)} %param.11, s32[1024]{0:T(1024)S(1)} %pad_clamp_fusion.1), kind=kCustom, calls=%fused_computation | custom fusion | bytes 787456 | tf_op jit(solution)/shard_map/jit(_take)/gather | solution.py:41
  58.2 0.9 fusion.2
  59.1 4.5 %all-to-all-start.1 = ((f32[32,8,3,128]{3,1,2,0:T(8,128)}), f32[32,8,3,128]{3,1,2,0:T(8,128)S(1)}, u32[]{:S(2)}, u32[]{:S(2)}) async-start(f32[32,8,3,128]{3,1,2,0:T(8,128)} %fusion.2), calls=%async_computation.1 | async-start | bytes 786432 | tf_op jit(solution)/shard_map/all_to_all | solution.py:42
  63.6 1.3 divide_multiply_fusion
  64.9 0.8 fusion.8
  65.7 0.8 convolution_add_fusion.1
  66.6 10.4 %all-to-all-done.1 = f32[32,8,3,128]{3,1,2,0:T(8,128)S(1)} async-done(((f32[32,8,3,128]{3,1,2,0:T(8,128)}), f32[32,8,3,128]{3,1,2,0:T(8,128)S(1)}, u32[]{:S(2)}, u32[]{:S(2)}) %all-to-all-start.1) | async-done | bytes 393248 | tf_op jit(solution)/shard_map/all_to_all | solution.py:42
  77.0 0.1 copy.34
  77.2 0.8 gather_fusion.1
  77.9 15.5 %convolution_multiply_fusion = f32[128,3,128]{2,1,0:T(4,128)S(1)} fusion(f32[128,128,128]{2,1,0:T(8,128)} %param.12, f32[128,3,128]{2,1,0:T(4,128)S(1)} %gather_fusion.1, pred[128]{0:T(512)(128)(4,1)S(1)} %get-tuple-element.4), kind=kOutput, calls=%fused_computation.3 | convolution fusion | flops 75595776 | bytes 8781952 | tf_op jit(solution)/shard_map/lij,lcj->lci/dot_general | solution.py:51
  93.4 0.0 copy-done.1
  93.4 0.0 copy-done.2
  93.4 0.0 copy-done.4
  93.4 0.2 fusion.1
  93.6 0.0 copy-start.3
  93.6 0.2 fusion.10
  93.8 0.0 copy-done.5
  93.8 0.2 fusion.17
  94.0 38.5 %psum.23 = f32[16,3]{0,1:T(4,128)S(1)} all-reduce(f32[16,3]{0,1:T(4,128)S(1)} %fusion.17), channel_id=1, replica_groups=mesh['grp'=4,'clu'=8] {'grp','clu'}, use_global_device_ids=true, to_apply=%region_7.8 | all-reduce | flops 48 | bytes 384 | tf_op jit(solution)/shard_map/psum | solution.py:82
  132.5 0.6 broadcast_divide_fusion
  133.1 0.0 copy-done.3
  (4 shorter events, 0.0 us)
Async XLA Ops:
  0.6 11.3 %copy-start = (f32[4,128]{1,0:T(4,128)S(1)}, f32[4,128]{1,0:T(4,128)}, u32[]{:S(2)}) copy-start(f32[4,128]{1,0:T(4,128)} %param.18) | copy-start | bytes 6148
  4.5 51.1 %all-to-all-start = ((s32[32,1,8]{2,1,0:T(1,128)}), s32[32,1,8]{2,1,0:T(1,128)S(1)}, u32[]{:S(2)}, u32[]{:S(2)}) async-start(s32[32,1,8]{2,1,0:T(1,128)} %bitcast.5), calls=%async_computation | async-start | bytes 32768 | tf_op jit(solution)/shard_map/all_to_all | solution.py:37
  56.1 37.3 %copy-start.1 = (f32[4,3,128]{2,0,1:T(4,128)S(1)}, f32[4,3,128]{2,0,1:T(4,128)}, u32[]{:S(2)}) copy-start(f32[4,3,128]{2,0,1:T(4,128)} %param.16) | copy-start | bytes 18436
  56.1 37.3 %copy-start.2 = (f32[4,3,128]{2,0,1:T(4,128)S(1)}, f32[4,3,128]{2,0,1:T(4,128)}, u32[]{:S(2)}) copy-start(f32[4,3,128]{2,0,1:T(4,128)} %param.17) | copy-start | bytes 18436
  56.1 37.3 %copy-start.4 = (s32[128]{0:T(128)S(1)}, s32[128]{0:T(128)}, u32[]{:S(2)}) copy-start(s32[128]{0:T(128)} %param.15) | copy-start | bytes 1540
  56.1 37.6 %copy-start.5 = (s32[4]{0:T(128)S(1)}, s32[4]{0:T(128)}, u32[]{:S(2)}) copy-start(s32[4]{0:T(128)} %param.19) | copy-start | bytes 52
  59.1 17.9 %all-to-all-start.1 = ((f32[32,8,3,128]{3,1,2,0:T(8,128)}), f32[32,8,3,128]{3,1,2,0:T(8,128)S(1)}, u32[]{:S(2)}, u32[]{:S(2)}) async-start(f32[32,8,3,128]{3,1,2,0:T(8,128)} %fusion.2), calls=%async_computation.1 | async-start | bytes 786432 | tf_op jit(solution)/shard_map/all_to_all | solution.py:42
  93.6 39.5 %copy-start.3 = (f32[4,3,128]{2,0,1:T(4,128)}, f32[4,3,128]{2,0,1:T(4,128)S(1)}, u32[]{:S(2)}) copy-start(f32[4,3,128]{2,0,1:T(4,128)S(1)} %fusion.1) | copy-start | bytes 18436
where the time goes:
time: 134 us; the launch traced here: 133 us
  blocking collectives  79 us (59%)
  matrix products  20.2 us (15%)
  starting transfers between devices  11.8 us (9%)
  waiting for transfers between devices  10.4 us (8%)
  other arithmetic  5.86 us (4%)
  local copies, waits for them, and re-layouts  5.07 us (4%)
    psum x1, blocking collectives, on_device(): group_sum, group_area = lax.psum((local_sum, local_area), ('grp', 'clu'))  40.4 us
    psum x1, blocking collectives, on_device(): new_sum = lax.psum(new_local, ('grp', 'clu'))  38.5 us
    dot_general x1, matrix products, on_device(): jnp.einsum('lij,lcj->lci', form_factors, fetched, precision=lax.Precision...  15.5 us
    all_to_all x1, waiting for transfers between devices, on_device(): lax.all_to_all(answer.reshape(devices, capacity, 3, width), ('grp', 'clu'...  10.4 us
    all_to_all x1, starting transfers between devices, on_device(): lax.all_to_all(wanted.reshape(devices, capacity), ('grp', 'clu'), split_a...  7.33 us
    all_to_all x1, starting transfers between devices, on_device(): lax.all_to_all(answer.reshape(devices, capacity, 3, width), ('grp', 'clu'...  4.48 us
  transfers between devices with their start and end apart: 2, of which 1 were waited for; matrix products, arithmetic and copies ran while one was open for 5% of the time, Pallas kernels for 0%

commit v1 on v0

--- a/solution.py
+++ b/solution.py
@@ -79,7 +79,7 @@
     new_local = jnp.dot(
         group_table.T, cluster_sums(radiosity_new, patch_area), precision=lax.Precision.HIGHEST
     )
-    new_sum = lax.psum(new_local, ("grp", "clu"))
+    new_sum = jnp.sum(lax.all_gather(new_local, ("grp", "clu")), axis=0)
     return (radiosity_new, new_sum / group_area[:, None])
 
 

time: 134 us -> 160 us (1.19)
  blocking collectives: 79 us -> 105 us
    all_gather x0 -> x1, blocking collectives: none -> 64.8 us  [on_device(): new_sum = jnp.sum(lax.all_gather(new_local, ('grp', 'clu')), axis=0)]
    psum x1 -> x0, blocking collectives: 38.5 us -> none  [on_device(): new_sum = lax.psum(new_local, ('grp', 'clu'))]
  transfers between devices with their start and end apart: 2 -> 2, of which waited for: 1 -> 1; matrix products, arithmetic and copies ran while one was open for 5% -> 4% of each run, Pallas kernels for 0% -> 0%
where the time goes in v1:
time: 160 us; the launch traced here: 159 us
  blocking collectives  105 us (66%)
  matrix products  20.2 us (13%)
  starting transfers between devices  11.8 us (7%)
  waiting for transfers between devices  10.4 us (6%)
  other arithmetic  5.91 us (4%)
  local copies, waits for them, and re-layouts  5.07 us (3%)
    all_gather x1, blocking collectives, on_device(): new_sum = jnp.sum(lax.all_gather(new_local, ('grp', 'clu')), axis=0)  64.8 us
    psum x1, blocking collectives, on_device(): group_sum, group_area = lax.psum((local_sum, local_area), ('grp', 'clu'))  40.4 us
    dot_general x1, matrix products, on_device(): jnp.einsum('lij,lcj->lci', form_factors, fetched, precision=lax.Precision...  15.5 us
    all_to_all x1, waiting for transfers between devices, on_device(): lax.all_to_all(answer.reshape(devices, capacity, 3, width), ('grp', 'clu'...  10.4 us
    all_to_all x1, starting transfers between devices, on_device(): lax.all_to_all(wanted.reshape(devices, capacity), ('grp', 'clu'), split_a...  7.33 us
    all_to_all x1, starting transfers between devices, on_device(): lax.all_to_all(answer.reshape(devices, capacity, 3, width), ('grp', 'clu'...  4.48 us
  transfers between devices with their start and end apart: 2, of which 1 were waited for; matrix products, arithmetic and copies ran while one was open for 4% of the time, Pallas kernels for 0%

profile of v1, /device:TPU:0, one launch (start us, length us, event | category | flops | bytes accessed | tf_op | source)
XLA Modules:
  0.0 159.4 jit_solution(7445795342412630782)
XLA Ops:
  0.6 0.0 copy-start
  0.6 0.9 convert_reduce_fusion
  1.6 0.7 and_bitcast_fusion
  2.2 0.7 broadcast_add_fusion
  2.9 1.0 scatter_custom_fusion
  3.9 0.7 all_to_all.9
  4.5 7.3 %all-to-all-start = ((s32[32,1,8]{2,1,0:T(1,128)}), s32[32,1,8]{2,1,0:T(1,128)S(1)}, u32[]{:S(2)}, u32[]{:S(2)}) async-start(s32[32,1,8]{2,1,0:T(1,128)} %bitcast.5), calls=%async_computation | async-start | bytes 32768 | tf_op jit(solution)/shard_map/all_to_all | solution.py:37
  11.9 0.0 copy-done
  11.9 0.1 reduce_sum.49
  12.0 0.8 fusion.12
  12.9 0.9 fusion.17
  13.7 0.8 convolution_bitcast_fusion.1
  14.5 40.4 %all-reduce = (f32[16,3]{0,1:T(4,128)S(1)}, f32[16]{0:T(128)S(1)}) all-reduce(f32[16,3]{0,1:T(4,128)S(1)} %fusion.17, f32[16]{0:T(128)S(1)} %convolution_bitcast_fusion.1), channel_id=1, replica_groups=mesh['grp'=4,'clu'=8] {'grp','clu'}, use_global_device_ids=true, to_apply=%region_2.3 | all-reduce | flops 64 | bytes 512 | tf_op jit(solution)/shard_map/psum | solution.py:68
  54.9 0.6 reduce_sum.51
  55.5 0.1 reduce_sum.50
  55.7 0.0 all-to-all-done
  55.7 0.1 copy.28
  55.7 0.1 copy.33
  55.8 0.1 copy.29
  55.9 0.1 copy.30
  56.0 0.1 reshape.76
  56.1 0.0 copy-start.1
  56.1 0.0 copy-start.2
  56.1 0.0 copy-start.4
  56.1 0.0 copy-start.5
  56.1 2.1 %gather_fusion = f32[256,3,128]{2,0,1:T(8,128)S(1)} fusion(f32[4,3,128]{2,0,1:T(4,128)} %param.11, s32[1024]{0:T(1024)S(1)} %pad_clamp_fusion.1), kind=kCustom, calls=%fused_computation | custom fusion | bytes 787456 | tf_op jit(solution)/shard_map/jit(_take)/gather | solution.py:41
  58.2 0.9 fusion.2
  59.1 4.5 %all-to-all-start.1 = ((f32[32,8,3,128]{3,1,2,0:T(8,128)}), f32[32,8,3,128]{3,1,2,0:T(8,128)S(1)}, u32[]{:S(2)}, u32[]{:S(2)}) async-start(f32[32,8,3,128]{3,1,2,0:T(8,128)} %fusion.2), calls=%async_computation.1 | async-start | bytes 786432 | tf_op jit(solution)/shard_map/all_to_all | solution.py:42
  63.6 1.3 divide_multiply_fusion
  64.9 0.8 fusion.8
  65.7 0.8 convolution_add_fusion.1
  66.6 10.4 %all-to-all-done.1 = f32[32,8,3,128]{3,1,2,0:T(8,128)S(1)} async-done(((f32[32,8,3,128]{3,1,2,0:T(8,128)}), f32[32,8,3,128]{3,1,2,0:T(8,128)S(1)}, u32[]{:S(2)}, u32[]{:S(2)}) %all-to-all-start.1) | async-done | bytes 393248 | tf_op jit(solution)/shard_map/all_to_all | solution.py:42
  77.0 0.1 copy.34
  77.2 0.8 gather_fusion.1
  77.9 15.5 %convolution_multiply_fusion = f32[128,3,128]{2,1,0:T(4,128)S(1)} fusion(f32[128,128,128]{2,1,0:T(8,128)} %param.12, f32[128,3,128]{2,1,0:T(4,128)S(1)} %gather_fusion.1, pred[128]{0:T(512)(128)(4,1)S(1)} %get-tuple-element.4), kind=kOutput, calls=%fused_computation.3 | convolution fusion | flops 75595776 | bytes 8781952 | tf_op jit(solution)/shard_map/lij,lcj->lci/dot_general | solution.py:51
  93.4 0.0 copy-done.1
  93.4 0.0 copy-done.2
  93.4 0.0 copy-done.4
  93.4 0.2 fusion.1
  93.6 0.0 copy-start.3
  93.6 0.2 fusion.10
  93.8 0.0 copy-done.5
  93.8 0.2 convolution_bitcast_fusion
  94.0 64.8 %all-gather.1 = f32[32,16,3]{1,2,0:T(4,128)S(1)} all-gather(f32[1,16,3]{1,2,0:T(4,128)S(1)} %convolution_bitcast_fusion), channel_id=2, replica_groups=mesh['grp'=4,'clu'=8] {'grp','clu'}, dimensions={0}, use_global_device_ids=true | all-gather | bytes 6336 | tf_op jit(solution)/shard_map/all_gather | solution.py:82
  158.8 0.6 broadcast_divide_fusion
  159.4 0.0 copy-done.3
  (5 shorter events, 0.1 us)
Async XLA Ops:
  0.6 11.3 %copy-start = (f32[4,128]{1,0:T(4,128)S(1)}, f32[4,128]{1,0:T(4,128)}, u32[]{:S(2)}) copy-start(f32[4,128]{1,0:T(4,128)} %param.18) | copy-start | bytes 6148
  4.5 51.1 %all-to-all-start = ((s32[32,1,8]{2,1,0:T(1,128)}), s32[32,1,8]{2,1,0:T(1,128)S(1)}, u32[]{:S(2)}, u32[]{:S(2)}) async-start(s32[32,1,8]{2,1,0:T(1,128)} %bitcast.5), calls=%async_computation | async-start | bytes 32768 | tf_op jit(solution)/shard_map/all_to_all | solution.py:37
  56.1 37.3 %copy-start.1 = (f32[4,3,128]{2,0,1:T(4,128)S(1)}, f32[4,3,128]{2,0,1:T(4,128)}, u32[]{:S(2)}) copy-start(f32[4,3,128]{2,0,1:T(4,128)} %param.16) | copy-start | bytes 18436
  56.1 37.3 %copy-start.2 = (f32[4,3,128]{2,0,1:T(4,128)S(1)}, f32[4,3,128]{2,0,1:T(4,128)}, u32[]{:S(2)}) copy-start(f32[4,3,128]{2,0,1:T(4,128)} %param.17) | copy-start | bytes 18436
  56.1 37.3 %copy-start.4 = (s32[128]{0:T(128)S(1)}, s32[128]{0:T(128)}, u32[]{:S(2)}) copy-start(s32[128]{0:T(128)} %param.15) | copy-start | bytes 1540
  56.1 37.6 %copy-start.5 = (s32[4]{0:T(128)S(1)}, s32[4]{0:T(128)}, u32[]{:S(2)}) copy-start(s32[4]{0:T(128)} %param.19) | copy-start | bytes 52
  59.1 17.9 %all-to-all-start.1 = ((f32[32,8,3,128]{3,1,2,0:T(8,128)}), f32[32,8,3,128]{3,1,2,0:T(8,128)S(1)}, u32[]{:S(2)}, u32[]{:S(2)}) async-start(f32[32,8,3,128]{3,1,2,0:T(8,128)} %fusion.2), calls=%async_computation.1 | async-start | bytes 786432 | tf_op jit(solution)/shard_map/all_to_all | solution.py:42
  93.6 65.8 %copy-start.3 = (f32[4,3,128]{2,0,1:T(4,128)}, f32[4,3,128]{2,0,1:T(4,128)S(1)}, u32[]{:S(2)}) copy-start(f32[4,3,128]{2,0,1:T(4,128)S(1)} %fusion.1) | copy-start | bytes 18436
